TPU v7x, 32 devices: a whole 2x2x4 slice. The times are simulated.
32 devices in a mesh: date: 8 (over z, x), pix: 4 (over y, core).
Axes of the slice: x: 2, y: 2, z: 4, core: 2. Of those that a mesh axis runs over, the one named last changes fastest.
Arguments:
- stack: bfloat16 [8, 10, 32, 2048], P('date', None, 'pix'), may hold values from -4 to 12
- cloud: int32 [8, 32, 2048], P('date', 'pix'), may hold values 0 or 1
Outputs:
- composite: float32 [10, 32, 2048], P(None, 'pix')
All inputs are finite; a program needn't handle non-finite values. No bound on the sum of `cloud` on one device may be relied on, other than what follows from the above.
Results may differ from a plain program's by a relative error of at most 0.0003.
Values may be sent and summed in bfloat16 or wider, within the bound.
No kernel may reach another device: no remote copies, remote signals or barrier semaphores. Data moves between devices by JAX's collectives and lax.ppermute only.
A program may use at most 64 MiB of HBM per device.

v0:
```python
import jax
import jax.numpy as jnp
from jax import lax
from jax.sharding import PartitionSpec as P

ITERS = 2
delta_sq = 0.01
eps = 1e-05


def with_halo(cells, axis, dim):
    count = lax.axis_size(axis)
    ends = count - 1
    head = lax.slice_in_dim(cells, 0, 1, axis=dim)
    tail = lax.slice_in_dim(cells, cells.shape[dim] - 1, cells.shape[dim], axis=dim)
    return jnp.concatenate(
        [
            lax.ppermute(tail, axis, [(i, (i + 1) % count) for i in range(ends)]),
            cells,
            lax.ppermute(head, axis, [((i + 1) % count, i) for i in range(ends)]),
        ],
        axis=dim,
    )


def weiszfeld(values, valid):
    median = jnp.zeros(values.shape[1:], jnp.float32)
    for step in range(ITERS + 1):
        if step == 0:
            weight = valid
        else:
            diff = values - median[None]
            weight = valid / jnp.sqrt(jnp.sum(diff * diff, axis=1) + delta_sq)
        numer = jnp.sum(weight[:, None] * values, axis=0)
        denom = jnp.sum(weight, axis=0)
        median = (numer + median) / (denom + 1.0)
    return median


def body(stack, cloud):
    bands = stack.shape[1]
    rows = stack.shape[2]
    cols = stack.shape[3]
    cloudy = (1 - cloud).astype(jnp.bfloat16)
    rimmed = with_halo(cloudy, "pix", 1).astype(jnp.float32)
    padded = jnp.pad(rimmed, ((0, 0), (0, 0), (1, 1)))
    near = jnp.maximum(padded[:, 1:-1, 1:-1], padded[:, 2:, 1:-1])
    near = jnp.maximum(near, padded[:, :-2, 1:-1])
    near = jnp.maximum(near, padded[:, 1:-1, 2:])
    near = jnp.maximum(near, padded[:, 1:-1, :-2])
    valid = (1.0 - near).astype(jnp.bfloat16)
    planes = jnp.concatenate([stack, valid[:, None]], axis=1)
    planes = lax.all_to_all(planes, "date", 3, 0, tiled=True).astype(jnp.float32)
    median = weiszfeld(planes[:, :bands], planes[:, bands])
    median = lax.all_gather(median, "date", axis=2, tiled=True)
    count = lax.axis_size("pix") * rows * cols
    sums = lax.psum((jnp.sum(median, axis=(1, 2)), jnp.sum(median * median, axis=(1, 2))), "pix")
    mean = sums[0] / count
    var = sums[1] / count - mean * mean
    return (median - mean[:, None, None]) / jnp.sqrt(var[:, None, None] + eps)


def solution(mesh):
    placed = (P("date", None, "pix", None), P("date", "pix", None))
    return jax.shard_map(
        body, mesh=mesh, in_specs=placed, out_specs=P(None, "pix", None), check_vma=False
    )
```

profile of v0, /device:TPU:0, one launch (start us, length us, event | category | flops | bytes accessed | tf_op | source)
XLA Modules:
  0.0 144.7 jit_solution(4334048969689377763)
XLA Ops:
  0.0 0.8 subtract_convert_fusion
  0.9 2.4 %collective-permute-start = (bf16[1,1,2048]{2,1,0:T(2,128)(2,1)S(1)}, bf16[1,1,2048]{2,1,0:T(2,128)(2,1)S(1)}, u32[]{:S(2)}, u32[]{:S(2)}) collective-permute-start(bf16[1,1,2048]{2,1,0:T(2,128)(2,1)S(1)} %get-tuple-element.11), channel_id=1, source_target_pairs={{0,1},{1,2},{2,3},{4,5},{5,6},{6,7},{8,9},{9,10},{10,11},{12,13},{... | collective-permute-start | bytes 12296 | tf_op jit(solution)/shard_map/ppermute | solution.py:18
  3.3 1.3 collective-permute-start.1
  4.6 0.0 collective-permute-done
  4.6 3.9 %collective-permute-done.1 = bf16[1,1,2048]{2,1,0:T(2,128)(2,1)S(1)} collective-permute-done((bf16[1,1,2048]{2,1,0:T(2,128)(2,1)S(1)}, bf16[1,1,2048]{2,1,0:T(2,128)(2,1)S(1)}, u32[]{:S(2)}, u32[]{:S(2)}) %collective-permute-start.1) | collective-permute-done | bytes 4128 | tf_op jit(solution)/shard_map/ppermute | solution.py:20
  8.5 0.1 fusion.6
  8.6 1.0 pad_maximum_fusion
  9.6 4.3 %copy.33 = bf16[1,11,8,2048]{1,2,0,3:T(8,128)(2,1)} copy(bf16[1,11,8,2048]{3,2,1,0:T(8,128)(2,1)S(1)} %pad_maximum_fusion) | data formatting | bytes 720896 | tf_op jit(solution)/shard_map/concatenate | solution.py:52
  14.0 7.3 %reshape.94 = bf16[8,2,11264]{2,1,0:T(2,128)(2,1)S(1)} reshape(bf16[2048,1,8,11]{3,2,1,0:T(8,128)(2,1)} %bitcast.38) | data formatting | bytes 720896
  21.2 16.5 %all_to_all.4 = bf16[8,2,11264]{2,1,0:T(2,128)(2,1)S(1)} all-to-all(bf16[8,2,11264]{2,1,0:T(2,128)(2,1)S(1)} %reshape.94), channel_id=1, replica_groups=mesh['date'=8,'pix'=4] {'date'}, dimensions={0} | all-to-all | bytes 720896 | tf_op jit(solution)/shard_map/all_to_all | solution.py:53
  37.7 10.2 %reshape.95 = bf16[2048,1,8,11]{3,2,1,0:T(8,128)(2,1)} reshape(bf16[8,2,11264]{2,1,0:T(2,128)(2,1)S(1)} %all_to_all.4) | data formatting | bytes 720896
  47.9 17.2 %copy.34 = f32[1,11,8,8,256]{2,4,3,1,0:T(8,128)} copy(bf16[1,11,8,8,256]{1,2,4,3,0:T(8,128)(2,1)} %bitcast.39) | data formatting | bytes 1081344 | tf_op jit(solution)/shard_map/convert_element_type | solution.py:53
  65.1 1.4 fusion.8
  66.5 1.0 reduce_sum.91
  67.6 0.1 copy.37
  67.6 5.6 %multiply_reduce_fusion.4 = f32[10,8,256]{1,2,0:T(8,128)S(1)} fusion(f32[8,11,8,256]{2,3,0,1:T(8,128)} %bitcast.27, f32[8,8,256]{1,2,0:T(8,128)S(1)} %get-tuple-element.10), kind=kLoop, calls=%fused_computation.4 | loop fusion | flops 307200 | bytes 802816 | tf_op jit(solution)/shard_map/reduce_sum | solution.py:34
  73.2 0.4 copy.38
  73.6 0.4 copy.39
  74.0 5.6 %multiply_reduce_fusion.3 = f32[8,8,256]{1,2,0:T(8,128)S(1)} fusion(f32[8,11,8,256]{2,3,0,1:T(8,128)} %bitcast.28, f32[10,8,256]{1,2,0:T(8,128)S(1)} %copy.39), kind=kLoop, calls=%fused_computation.3 | loop fusion | flops 475136 | bytes 802816 | tf_op jit(solution)/shard_map/reduce_sum | solution.py:33
  79.6 1.5 %multiply_reduce_fusion.6 = f32[8,256]{0,1:T(8,128)S(1)} fusion(f32[8,8,256]{1,2,0:T(8,128)S(1)} %multiply_reduce_fusion.3, f32[8,11,8,256]{2,3,0,1:T(8,128)} %bitcast.29), kind=kLoop, calls=%fused_computation.11 | loop fusion | flops 47104 | bytes 139264 | tf_op jit(solution)/shard_map/reduce_sum | solution.py:35
  81.0 1.5 %fusion.1 = f32[8,8,256]{1,2,0:T(8,128)S(1)} fusion(f32[8,8,256]{1,2,0:T(8,128)S(1)} %multiply_reduce_fusion.3, f32[8,11,8,256]{2,3,0,1:T(8,128)} %bitcast.30), kind=kLoop, calls=%fused_computation.8 | loop fusion | flops 32768 | bytes 196608 | tf_op jit(solution)/shard_map/mul | solution.py:34
  82.5 0.1 copy.42
  82.6 6.6 %multiply_reduce_fusion.2 = f32[10,8,256]{1,2,0:T(8,128)} fusion(f32[8,11,8,256]{2,3,0,1:T(8,128)} %bitcast.31, f32[8,8,256]{1,2,0:T(8,128)S(1)} %fusion.1), kind=kLoop, calls=%fused_computation.2 | loop fusion | flops 307200 | bytes 802816 | tf_op jit(solution)/shard_map/reduce_sum | solution.py:34
  89.2 0.0 slice-start
  89.2 1.8 %copy.41 = f32[10,8,256]{2,1,0:T(8,128)S(1)} copy(f32[10,8,256]{1,2,0:T(8,128)} %multiply_reduce_fusion.2) | data formatting | bytes 163840 | tf_op jit(solution)/shard_map/reduce_sum | solution.py:34
  91.1 1.5 %copy.43 = f32[10,8,256]{1,2,0:T(8,128)} copy(f32[10,8,256]{2,1,0:T(8,128)S(1)} %add_divide_fusion.1) | data formatting | bytes 163840 | tf_op jit(solution)/shard_map/div | solution.py:36
  92.6 0.0 slice-start.1
  92.6 0.0 slice-start.2
  92.6 6.1 %multiply_reduce_fusion.1 = f32[8,8,256]{1,2,0:T(8,128)S(1)} fusion(f32[8,11,8,256]{2,3,0,1:T(8,128)} %bitcast.32, f32[10,8,256]{1,2,0:T(8,128)} %copy.43), kind=kLoop, calls=%fused_computation.1 | loop fusion | flops 475136 | bytes 802816 | tf_op jit(solution)/shard_map/reduce_sum | solution.py:33
  98.7 1.5 %multiply_reduce_fusion.5 = f32[8,256]{0,1:T(8,128)S(1)} fusion(f32[8,8,256]{1,2,0:T(8,128)S(1)} %multiply_reduce_fusion.1, f32[8,11,8,256]{2,3,0,1:T(8,128)} %bitcast.33), kind=kLoop, calls=%fused_computation.9 | loop fusion | flops 47104 | bytes 139264 | tf_op jit(solution)/shard_map/reduce_sum | solution.py:35
  100.1 1.5 %fusion = f32[8,8,256]{1,2,0:T(8,128)S(1)} fusion(f32[8,8,256]{1,2,0:T(8,128)S(1)} %multiply_reduce_fusion.1, f32[8,11,8,256]{2,3,0,1:T(8,128)} %bitcast.34), kind=kLoop, calls=%fused_computation.6 | loop fusion | flops 32768 | bytes 196608 | tf_op jit(solution)/shard_map/mul | solution.py:34
  101.6 0.0 slice-done
  101.6 0.0 slice-done.1
  101.6 0.0 slice-done.2
  101.6 2.5 %multiply_reduce_fusion = f32[10,8,256]{1,2,0:T(8,128)} fusion(f32[8,11,8,256]{2,3,0,1:T(8,128)S(1)} %bitcast.37, f32[8,8,256]{1,2,0:T(8,128)S(1)} %fusion), kind=kLoop, calls=%fused_computation | loop fusion | flops 307200 | bytes 802816 | tf_op jit(solution)/shard_map/reduce_sum | solution.py:34
  104.1 1.7 %copy.45 = f32[10,8,256]{2,1,0:T(8,128)S(1)} copy(f32[10,8,256]{1,2,0:T(8,128)} %multiply_reduce_fusion) | data formatting | bytes 163840 | tf_op jit(solution)/shard_map/reduce_sum | solution.py:34
  105.8 0.1 copy.46
  105.9 32.0 %all_gather.3 = f32[10,8,2048]{2,1,0:T(8,128)S(1)} all-gather(f32[10,8,256]{2,1,0:T(8,128)S(1)} %add_divide_fusion), channel_id=1, replica_groups=mesh['date'=8,'pix'=4] {'date'}, dimensions={2}, use_global_device_ids=true | all-gather | bytes 737280 | tf_op jit(solution)/shard_map/all_gather | solution.py:55
  137.9 0.2 fusion.7
  138.1 5.7 %all-reduce.1 = (f32[10]{0:T(128)S(1)}, f32[10]{0:T(128)S(1)}) all-reduce(f32[10]{0:T(128)S(1)} %get-tuple-element.6, f32[10]{0:T(128)S(1)} %get-tuple-element.5), channel_id=1, replica_groups=mesh['date'=8,'pix'=4] {'pix'}, use_global_device_ids=true, to_apply=%region_11.12 | all-reduce | flops 20 | bytes 160 | tf_op jit(solution)/shard_map/psum | solution.py:57
  143.7 1.0 subtract_divide_fusion
  (10 shorter events, 0.2 us)
Async XLA Ops:
  0.9 3.7 %collective-permute-start = (bf16[1,1,2048]{2,1,0:T(2,128)(2,1)S(1)}, bf16[1,1,2048]{2,1,0:T(2,128)(2,1)S(1)}, u32[]{:S(2)}, u32[]{:S(2)}) collective-permute-start(bf16[1,1,2048]{2,1,0:T(2,128)(2,1)S(1)} %get-tuple-element.11), channel_id=1, source_target_pairs={{0,1},{1,2},{2,3},{4,5},{5,6},{6,7},{8,9},{9,10},{10,11},{12,13},{... | collective-permute-start | bytes 12296 | tf_op jit(solution)/shard_map/ppermute | solution.py:18
  3.3 5.2 %collective-permute-start.1 = (bf16[1,1,2048]{2,1,0:T(2,128)(2,1)S(1)}, bf16[1,1,2048]{2,1,0:T(2,128)(2,1)S(1)}, u32[]{:S(2)}, u32[]{:S(2)}) collective-permute-start(bf16[1,1,2048]{2,1,0:T(2,128)(2,1)S(1)} %get-tuple-element.12), channel_id=1, source_target_pairs={{1,0},{2,1},{3,2},{5,4},{6,5},{7,6},{9,8},{10,9},{11,10},{13,12},{... | collective-permute-start | bytes 12296 | tf_op jit(solution)/shard_map/ppermute | solution.py:20
  89.2 12.4 %slice-start = ((s8[11534336]{0:T(1024)(128)(4,1)}), s8[3145728]{0:T(1024)(128)(4,1)S(1)}, s32[]{:S(2)}) async-start(s8[11534336]{0:T(1024)(128)(4,1)} %bitcast.35), calls=%async_computation.1 | async-start | bytes 6291456
  92.6 9.1 %slice-start.1 = ((s8[11534336]{0:T(1024)(128)(4,1)}), s8[4194304]{0:T(1024)(128)(4,1)S(1)}, s32[]{:S(2)}) async-start(s8[11534336]{0:T(1024)(128)(4,1)} %bitcast.35), calls=%async_computation.2 | async-start | bytes 8388608
  92.6 9.1 %slice-start.2 = ((s8[11534336]{0:T(1024)(128)(4,1)}), s8[4194304]{0:T(1024)(128)(4,1)S(1)}, s32[]{:S(2)}) async-start(s8[11534336]{0:T(1024)(128)(4,1)} %bitcast.35), calls=%async_computation.3 | async-start | bytes 8388608
where the time goes:
time: 145 us
  blocking collectives  54.1 us (37%)
  local copies, waits for them, and re-layouts  46.4 us (32%)
  other arithmetic  36.5 us (25%)
  waiting for transfers between devices  3.88 us (3%)
  starting transfers between devices  3.69 us (3%)
    all_gather x1, blocking collectives, body(): median = lax.all_gather(median, 'date', axis=2, tiled=True)  32 us
    unnamed x8, local copies, waits for them, and re-layouts  17.5 us
    convert_element_type x1, local copies, waits for them, and re-layouts, body(): lax.all_to_all(planes, 'date', 3, 0, tiled=True).astype(jnp.float32)  17.2 us
    all_to_all x1, blocking collectives, body(): lax.all_to_all(planes, 'date', 3, 0, tiled=True).astype(jnp.float32)  16.5 us
    reduce_sum x3, other arithmetic, weiszfeld(): numer = jnp.sum(weight[:, None] * values, axis=0)  14.6 us
    reduce_sum x2, other arithmetic, weiszfeld(): weight = valid / jnp.sqrt(jnp.sum(diff * diff, axis=1) + delta_sq)  11.7 us
    psum x1, blocking collectives, body(): lax.psum((jnp.sum(median, axis=(1, 2)), jnp.sum(median * median, axis=(1,...  5.66 us
    concatenate x1, local copies, waits for them, and re-layouts, body(): planes = jnp.concatenate([stack, valid[:, None]], axis=1)  4.35 us
  transfers between devices with their start and end apart: 2, of which 1 were waited for; matrix products, arithmetic and copies ran while one was open for 0% of the time, Pallas kernels for 0%

commit v1 on v0

--- a/solution.py
+++ b/solution.py
@@ -50,7 +50,10 @@
     near = jnp.maximum(near, padded[:, 1:-1, :-2])
     valid = (1.0 - near).astype(jnp.bfloat16)
     planes = jnp.concatenate([stack, valid[:, None]], axis=1)
-    planes = lax.all_to_all(planes, "date", 3, 0, tiled=True).astype(jnp.float32)
+    planes = jnp.concatenate(
+        lax.all_to_all(jnp.stack(jnp.split(planes, lax.axis_size("date"), axis=3)), "date", 0, 0),
+        axis=0,
+    ).astype(jnp.float32)
     median = weiszfeld(planes[:, :bands], planes[:, bands])
     median = lax.all_gather(median, "date", axis=2, tiled=True)
     count = lax.axis_size("pix") * rows * cols

time: 145 us -> 64.9 us (0.45)
  local copies, waits for them, and re-layouts: 46.4 us -> 0.02 us
  other arithmetic: 36.5 us -> 2.77 us
    unnamed x8 -> x2, local copies, waits for them, and re-layouts: 17.5 us -> 0.01 us
    convert_element_type x1 -> x0, local copies, waits for them, and re-layouts: 17.2 us -> none  [body(): lax.all_to_all(planes, 'date', 3, 0, tiled=True).astype(jnp.float32)]
    reduce_sum x3, other arithmetic: 14.6 us -> 0.16 us  [weiszfeld(): numer = jnp.sum(weight[:, None] * values, axis=0)]
    reduce_sum x2, other arithmetic: 11.7 us -> 0.13 us  [weiszfeld(): weight = valid / jnp.sqrt(jnp.sum(diff * diff, axis=1) + delta_sq)]
    concatenate x1 -> x0, local copies, waits for them, and re-layouts: 4.35 us -> none  [body(): planes = jnp.concatenate([stack, valid[:, None]], axis=1)]
    reduce_sum x3, other arithmetic: 3.94 us -> 0.06 us  [weiszfeld(): denom = jnp.sum(weight, axis=0)]
    reduce_sum x3 -> x0, local copies, waits for them, and re-layouts: 3.86 us -> none  [weiszfeld(): numer = jnp.sum(weight[:, None] * values, axis=0)]
    mul x2, other arithmetic: 2.96 us -> 0.04 us  [weiszfeld(): numer = jnp.sum(weight[:, None] * values, axis=0)]
where the time goes in v1:
time: 64.9 us; the launch traced here: 64.7 us
  blocking collectives  54.1 us (83%)
  waiting for transfers between devices  3.88 us (6%)
  starting transfers between devices  3.69 us (6%)
  other arithmetic  2.77 us (4%)
    all_gather x1, blocking collectives, body(): median = lax.all_gather(median, 'date', axis=2, tiled=True)  32 us
    all_to_all x1, blocking collectives, body(): lax.all_to_all(jnp.stack(jnp.split(planes, lax.axis_size('date'), axis=3)...  16.5 us
    psum x1, blocking collectives, body(): lax.psum((jnp.sum(median, axis=(1, 2)), jnp.sum(median * median, axis=(1,...  5.66 us
    ppermute x1, waiting for transfers between devices, with_halo(): lax.ppermute(head, axis, [((i + 1) % count, i) for i in range(ends)])  3.88 us
    ppermute x1, starting transfers between devices, with_halo(): lax.ppermute(tail, axis, [(i, (i + 1) % count) for i in range(ends)])  2.4 us
  transfers between devices with their start and end apart: 2, of which 1 were waited for; matrix products, arithmetic and copies ran while one was open for 0% of the time, Pallas kernels for 0%

profile of v1, /device:TPU:0, one launch (start us, length us, event | category | flops | bytes accessed | tf_op | source)
XLA Modules:
  0.0 64.7 jit_solution(7232024814883453630)
XLA Ops:
  0.0 0.0 copy-start
  0.0 0.9 %subtract_convert_fusion = bf16[1,8,2048]{2,1,0:T(8,128)(2,1)S(1)} fusion(s32[1,8,2048]{2,1,0:T(8,128)} %param.3), kind=kLoop, calls=%fused_computation.41 | loop fusion | flops 32768 | bytes 98304 | tf_op jit(solution)/shard_map/convert_element_type | solution.py:44
  0.9 2.4 %collective-permute-start = (bf16[1,1,2048]{2,1,0:T(2,128)(2,1)S(1)}, bf16[1,1,2048]{2,1,0:T(2,128)(2,1)S(1)}, u32[]{:S(2)}, u32[]{:S(2)}) collective-permute-start(bf16[1,1,2048]{2,1,0:T(2,128)(2,1)S(1)} %get-tuple-element.11), channel_id=1, source_target_pairs={{0,1},{1,2},{2,3},{4,5},{5,6},{6,7},{8,9},{9,10},{10,11},{12,13},{... | collective-permute-start | bytes 12296 | tf_op jit(solution)/shard_map/ppermute | solution.py:18
  3.3 1.3 %collective-permute-start.1 = (bf16[1,1,2048]{2,1,0:T(2,128)(2,1)S(1)}, bf16[1,1,2048]{2,1,0:T(2,128)(2,1)S(1)}, u32[]{:S(2)}, u32[]{:S(2)}) collective-permute-start(bf16[1,1,2048]{2,1,0:T(2,128)(2,1)S(1)} %get-tuple-element.12), channel_id=1, source_target_pairs={{1,0},{2,1},{3,2},{5,4},{6,5},{7,6},{9,8},{10,9},{11,10},{13,12},{... | collective-permute-start | bytes 12296 | tf_op jit(solution)/shard_map/ppermute | solution.py:20
  4.6 0.0 collective-permute-done
  4.6 3.9 %collective-permute-done.1 = bf16[1,1,2048]{2,1,0:T(2,128)(2,1)S(1)} collective-permute-done((bf16[1,1,2048]{2,1,0:T(2,128)(2,1)S(1)}, bf16[1,1,2048]{2,1,0:T(2,128)(2,1)S(1)}, u32[]{:S(2)}, u32[]{:S(2)}) %collective-permute-start.1) | collective-permute-done | bytes 4128 | tf_op jit(solution)/shard_map/ppermute | solution.py:20
  8.5 0.1 fusion.15
  8.7 0.0 copy-done
  8.8 16.5 %all_to_all.5 = bf16[8,1,11,8,256]{4,3,2,1,0:T(8,128)(2,1)S(1)} all-to-all(bf16[8,1,11,8,256]{4,3,2,1,0:T(8,128)(2,1)S(1)} %fusion.14), channel_id=1, replica_groups=mesh['date'=8,'pix'=4] {'date'}, dimensions={0} | all-to-all | bytes 720896 | tf_op jit(solution)/shard_map/all_to_all | solution.py:54
  25.3 0.1 bitcast_convert_fusion
  25.3 0.1 multiply_reduce_fusion.5
  25.4 0.1 multiply_reduce_fusion.4
  25.6 0.1 multiply_reduce_fusion.3
  25.6 0.1 multiply_reduce_fusion.2
  25.8 0.1 multiply_reduce_fusion.1
  25.9 32.0 %all_gather.3 = f32[10,8,2048]{2,1,0:T(8,128)S(1)} all-gather(f32[10,8,256]{2,1,0:T(8,128)S(1)} %add_divide_fusion), channel_id=1, replica_groups=mesh['date'=8,'pix'=4] {'date'}, dimensions={2}, use_global_device_ids=true | all-gather | bytes 737280 | tf_op jit(solution)/shard_map/all_gather | solution.py:58
  57.8 0.2 fusion.16
  58.0 5.7 %all-reduce.1 = (f32[10]{0:T(128)S(1)}, f32[10]{0:T(128)S(1)}) all-reduce(f32[10]{0:T(128)S(1)} %get-tuple-element.6, f32[10]{0:T(128)S(1)} %get-tuple-element.5), channel_id=1, replica_groups=mesh['date'=8,'pix'=4] {'pix'}, use_global_device_ids=true, to_apply=%region_11.12 | all-reduce | flops 20 | bytes 160 | tf_op jit(solution)/shard_map/psum | solution.py:60
  63.7 1.0 %subtract_divide_fusion = f32[10,8,2048]{2,1,0:T(8,128)} fusion(f32[10,8,2048]{2,1,0:T(8,128)S(1)} %all_gather.3, f32[10]{0:T(128)S(1)} %get-tuple-element.14, f32[10]{0:T(128)S(1)} %get-tuple-element.13), kind=kLoop, calls=%fused_computation.8 | loop fusion | flops 327680 | bytes 1310800 | tf_op jit(solution)/shard_map/div | solution.py:63
  (22 shorter events, 0.3 us)
Async XLA Ops:
  0.0 8.7 %copy-start = (bf16[1,10,8,2048]{3,2,1,0:T(8,128)(2,1)S(1)}, bf16[1,10,8,2048]{3,2,1,0:T(8,128)(2,1)}, u32[]{:S(2)}) copy-start(bf16[1,10,8,2048]{3,2,1,0:T(8,128)(2,1)} %param.2) | copy-start | bytes 983044
  0.9 3.7 %collective-permute-start = (bf16[1,1,2048]{2,1,0:T(2,128)(2,1)S(1)}, bf16[1,1,2048]{2,1,0:T(2,128)(2,1)S(1)}, u32[]{:S(2)}, u32[]{:S(2)}) collective-permute-start(bf16[1,1,2048]{2,1,0:T(2,128)(2,1)S(1)} %get-tuple-element.11), channel_id=1, source_target_pairs={{0,1},{1,2},{2,3},{4,5},{5,6},{6,7},{8,9},{9,10},{10,11},{12,13},{... | collective-permute-start | bytes 12296 | tf_op jit(solution)/shard_map/ppermute | solution.py:18
  3.3 5.2 %collective-permute-start.1 = (bf16[1,1,2048]{2,1,0:T(2,128)(2,1)S(1)}, bf16[1,1,2048]{2,1,0:T(2,128)(2,1)S(1)}, u32[]{:S(2)}, u32[]{:S(2)}) collective-permute-start(bf16[1,1,2048]{2,1,0:T(2,128)(2,1)S(1)} %get-tuple-element.12), channel_id=1, source_target_pairs={{1,0},{2,1},{3,2},{5,4},{6,5},{7,6},{9,8},{10,9},{11,10},{13,12},{... | collective-permute-start | bytes 12296 | tf_op jit(solution)/shard_map/ppermute | solution.py:20
